TPU v7x, 768 devices: a whole 4x8x12 slice. The times are simulated.
768 devices in a mesh: dp: 24 (over z, x_hi), seq: 32 (over y, x_lo, core).
Axes of the slice: x: 4 (x_hi: 2, x_lo: 2; x = x_hi * 2 + x_lo), y: 8, z: 12, core: 2. Of those that a mesh axis runs over, the one named last changes fastest.
Arguments:
- projections: bfloat16 [1, 24, 4096, 4096], P(None, 'dp', 'seq'), may hold values from -6 to 6
- rotated_query_gradient: bfloat16 [1, 24, 4096, 4096], P(None, 'dp', None, 'seq'), may hold values from -6 to 6
- gains: float32 [1, 4096], replicated, may hold values from 0.25 to 1.75
- adapter_lowering: bfloat16 [1, 48, 5120], P(None, 'dp'), may hold values from -0.078125 to 0.078125
- adapter_raising: bfloat16 [1, 48, 4096], P(None, 'dp'), may hold values from -0.875 to 0.875
- activations: bfloat16 [24, 4096, 5120], P('dp', 'seq'), may hold values from -6 to 6
- positions: int32 [3, 24, 4096], P(None, 'dp', 'seq'), may hold values from 0 to 38, as said below
- valid: int32 [24, 4096], P('dp', 'seq'), may hold values from 0 to 1, as said below
Outputs:
- grad_down: float32 [1, 48, 5120], P(None, 'dp')
- grad_up: float32 [1, 48, 4096], P(None, 'dp')
- grad_gain: float32 [1, 4096], replicated
Inputs may be any that keep to these rules, and one draw needn't show every extreme that they name: `positions`: within a video the frame index never falls; one frame holds 128 tokens. Every eighth token of a video is valid.
All inputs are finite; a program needn't handle non-finite values.
Results may differ from a plain program's by a relative error of at most 0.0041.
Values may be sent and summed in bfloat16 or wider, within the bound.
No kernel may reach another device: no remote copies, remote signals or barrier semaphores. Data moves between devices by JAX's collectives and lax.ppermute only.
A program may use at most 32 MiB of HBM per device.

v0:
```python
import jax
import jax.numpy as jnp
from jax import lax
from jax.sharding import PartitionSpec as P

HD = 128


EPSILON = 1e-06


def cut_along(x, dim, count):
    lengths = x.shape
    blocks = x.reshape(*lengths[:dim], count, lengths[dim] // count, *lengths[dim + 1 :])
    return jnp.moveaxis(blocks, dim, 0)


def summed_on_arrival(x, axis, dim):
    count = lax.axis_size(axis)
    blocks = lax.all_to_all(cut_along(x, dim, count), axis, 0, 0, tiled=True)
    return jnp.sum(blocks, axis=0)


def side_by_side(arrays, axis, dim, along):
    both = jnp.concatenate(arrays, axis=along)
    filled, at, outs = (summed_on_arrival(both, axis, dim), 0, [])
    for a in arrays:
        outs.append(lax.slice_in_dim(filled, at, at + a.shape[along], axis=along))
        at += a.shape[along]
    return tuple(outs)


def packed_total(arrays, axis):
    ends = [0]
    for a in arrays:
        ends.append(ends[-1] + a.size)
    running = lax.psum(jnp.concatenate([a.ravel() for a in arrays]), axis)
    return tuple((running[b:e].reshape(a.shape) for a, b, e in zip(arrays, ends, ends[1:])))


def rope_tables(positions, head_size):
    one_sixth = head_size // 6
    counts = (head_size // 2 - 2 * one_sixth, one_sixth, one_sixth)
    pieces = []
    for component in range(3):
        frequency = 10000.0 ** (
            -jnp.arange(counts[component], dtype=jnp.float32) / counts[component]
        )
        pieces.append(positions[component].astype(jnp.float32)[..., None] * frequency)
    angles = jnp.concatenate(pieces, -1)
    return (jnp.cos(angles), jnp.sin(angles))


def norm_backward(projections, rotated_query_gradient, gains, positions, valid):
    cosine, sine_table = rope_tables(positions, HD)
    full_shape = rotated_query_gradient.shape
    cotangent = (
        rotated_query_gradient.astype(jnp.float32) * valid.astype(jnp.float32)[None, :, :, None]
    )
    cotangent = cotangent.reshape(full_shape[:3] + (full_shape[3] // HD, HD // 2, 2))
    cosine = cosine[None, :, :, None, :]
    sine_table = sine_table[None, :, :, None, :]
    even_part = cosine * cotangent[..., 0] + sine_table * cotangent[..., 1]
    odd_part = cosine * cotangent[..., 1] - sine_table * cotangent[..., 0]
    unrotated = jnp.stack([even_part, odd_part], -1).reshape(full_shape)
    values = projections.astype(jnp.float32)
    inverse = lax.rsqrt(jnp.mean(values * values, -1, keepdims=True) + EPSILON)
    normed = values * inverse
    gain_part = jnp.sum(unrotated * normed, axis=(1, 2))
    scaled = unrotated * gains[:, None, None, :]
    projection_change = inverse * (scaled - normed * jnp.mean(scaled * normed, -1, keepdims=True))
    return (projection_change.astype(jnp.bfloat16), gain_part)


def adapter_partial_terms(projection_change, input_list, lowering_matrices, raising_matrices):
    reduced = jnp.dot(
        input_list, lowering_matrices[0].T, preferred_element_type=jnp.float32
    ).astype(jnp.bfloat16)
    up_terms = [jnp.dot(reduced.T, projection_change[0], preferred_element_type=jnp.float32)]
    back_rank = jnp.dot(
        projection_change[0], raising_matrices[0].T, preferred_element_type=jnp.float32
    ).astype(jnp.bfloat16)
    down_terms = [jnp.dot(back_rank.T, input_list, preferred_element_type=jnp.float32)]
    return (jnp.stack(down_terms), jnp.stack(up_terms))


def shards(
    projections,
    rotated_query_gradient,
    gains,
    adapter_lowering,
    adapter_raising,
    activations,
    positions,
    valid,
):
    local_count = jnp.sum(valid.astype(jnp.float32))
    token_grad = lax.all_to_all(
        rotated_query_gradient, "seq", split_axis=2, concat_axis=3, tiled=True
    )
    lowering_complete, raising_complete = (
        lax.all_gather(adapter_lowering, "dp", axis=1, tiled=True),
        lax.all_gather(adapter_raising, "dp", axis=1, tiled=True),
    )
    projection_change, gain_part = norm_backward(projections, token_grad, gains, positions, valid)
    lowering_portion, raising_portion = adapter_partial_terms(
        projection_change[:, 0], activations[0], lowering_complete, raising_complete
    )
    down_share, up_share = (
        summed_on_arrival(lowering_portion, "seq", 2),
        summed_on_arrival(raising_portion, "seq", 2),
    )
    down_share, up_share = side_by_side((down_share, up_share), "dp", 1, 2)
    down_sum, up_sum = (
        lax.all_gather(down_share, "seq", axis=2, tiled=True),
        lax.all_gather(up_share, "seq", axis=2, tiled=True),
    )
    gain_total, total_count = packed_total((gain_part, local_count), ("dp", "seq"))
    all_tokens = lax.axis_size("dp") * lax.axis_size("seq") * valid.shape[1]
    factor = jnp.float32(all_tokens) / total_count
    return (factor * down_sum, factor * up_sum, factor * gain_total)


def solution(mesh):
    in_specs = (
        P(None, "dp", "seq", None),
        P(None, "dp", None, "seq"),
        P(),
        P(None, "dp", None),
        P(None, "dp", None),
        P("dp", "seq", None),
        P(None, "dp", "seq"),
        P("dp", "seq"),
    )
    out_specs = (P(None, "dp", None), P(None, "dp", None), P())
    return jax.shard_map(shards, mesh=mesh, in_specs=in_specs, out_specs=out_specs, check_vma=False)
```

profile of v0, /device:TPU:1, one launch (start us, length us, event | category | flops | bytes accessed | tf_op | source)
XLA Modules:
  0.0 451.6 jit_solution(6001235459959523705)
XLA Ops:
  0.6 3.2 copy.76
  4.3 22.4 %reduce.6 = bf16[4096,128]{1,0:T(8,128)(2,1)S(1)} reduce(bf16[4096,1,1,128]{3,2,1,0:T(2,128)(2,1)S(1)} %bitcast.85, bf16[]{:T(256)} %broadcast.194), dimensions={1,2}, to_apply=%bitcast.76.reduce_sub_computation | reduce | bytes 2097154
  26.7 1.2 reshape.387
  27.9 14.8 %all-to-all-start = ((bf16[32,2,8192]{2,1,0:T(2,128)(2,1)}), bf16[32,2,8192]{2,1,0:T(2,128)(2,1)}, u32[]{:S(2)}, u32[]{:S(2)}) async-start(bf16[32,2,8192]{2,1,0:T(2,128)(2,1)} %reshape.387), calls=%async_computation | async-start | bytes 2097152 | tf_op jit(solution)/shard_map/all_to_all | solution.py:98
  42.8 0.7 copy.55
  43.8 0.6 fusion.8
  44.4 68.8 %all_gather.13 = bf16[1,48,5120]{2,0,1:T(2,128)(2,1)} all-gather(bf16[1,2,5120]{2,0,1:T(2,128)(2,1)S(1)} %copy.59), channel_id=1, replica_groups=mesh['dp'=24,'seq'=32] {'dp'}, dimensions={1}, use_global_device_ids=true | all-gather | bytes 512000 | tf_op jit(solution)/shard_map/all_gather | solution.py:102
  113.3 4.3 reshape.388
  117.6 1.1 copy.52
  118.7 2.0 copy.53
  121.6 1.6 copy.54
  123.2 1.3 fusion.3
  124.5 0.7 fusion.7
  125.3 0.6 copy-done
  125.9 3.5 convolution_bitcast_fusion.1
  129.3 14.2 %all-to-all-start.2 = ((f32[32,1,48,128]{3,2,1,0:T(8,128)}), f32[32,1,48,128]{3,2,1,0:T(8,128)}, u32[]{:S(2)}, u32[]{:S(2)}) async-start(f32[32,1,48,128]{3,2,1,0:T(8,128)} %convolution_bitcast_fusion.1), calls=%async_computation.2 | async-start | bytes 1572864 | tf_op jit(solution)/shard_map/all_to_all | solution.py:20
  143.5 1.5 copy.57
  145.0 52.5 %all_gather.12 = bf16[1,48,4096]{2,0,1:T(2,128)(2,1)S(1)} all-gather(bf16[1,2,4096]{2,0,1:T(2,128)(2,1)S(1)} %copy.56), channel_id=1, replica_groups=mesh['dp'=24,'seq'=32] {'dp'}, dimensions={1}, use_global_device_ids=true | all-gather | bytes 409600 | tf_op jit(solution)/shard_map/all_gather | solution.py:103
  197.5 3.9 convolution_bitcast_fusion
  201.4 16.4 %all-to-all-start.1 = ((f32[32,1,48,160]{3,2,1,0:T(8,128)}), f32[32,1,48,160]{3,2,1,0:T(8,128)S(1)}, u32[]{:S(2)}, u32[]{:S(2)}) async-start(f32[32,1,48,160]{3,2,1,0:T(8,128)} %convolution_bitcast_fusion), calls=%async_computation.1 | async-start | bytes 3145728 | tf_op jit(solution)/shard_map/all_to_all | solution.py:20
  217.8 0.6 convert_reduce_fusion
  218.4 0.6 pad_maximum_fusion.3
  219.1 131.2 %psum.7 = f32[4097]{0:T(1024)S(1)} all-reduce(f32[4097]{0:T(1024)S(1)} %pad_maximum_fusion.3), channel_id=1, replica_groups=mesh['dp'=24,'seq'=32] {'dp','seq'}, use_global_device_ids=true, to_apply=%region_3.0 | all-reduce | flops 4097 | bytes 32776 | tf_op jit(solution)/shard_map/psum | solution.py:37
  351.4 1.2 reduce_sum.70
  352.8 0.7 pad_maximum_fusion.1
  353.5 4.6 %all-to-all-start.3 = ((f32[24,1,2,288]{3,2,1,0:T(2,128)}), f32[24,1,2,288]{3,2,1,0:T(2,128)S(1)}, u32[]{:S(2)}, u32[]{:S(2)}) async-start(f32[24,1,2,288]{3,2,1,0:T(2,128)} %pad_maximum_fusion.1), calls=%async_computation.3 | async-start | bytes 147456 | tf_op jit(solution)/shard_map/all_to_all | solution.py:20
  358.1 0.6 slice_multiply_fusion
  358.7 10.6 %all-to-all-done.3 = f32[24,1,2,288]{3,2,1,0:T(2,128)S(1)} async-done(((f32[24,1,2,288]{3,2,1,0:T(2,128)}), f32[24,1,2,288]{3,2,1,0:T(2,128)S(1)}, u32[]{:S(2)}, u32[]{:S(2)}) %all-to-all-start.3) | async-done | bytes 55328 | tf_op jit(solution)/shard_map/all_to_all | solution.py:20
  369.5 34.0 %all_gather.15 = f32[1,2,4096]{2,1,0:T(2,128)S(1)} all-gather(f32[1,2,128]{2,1,0:T(2,128)S(1)} %slice.42), channel_id=1, replica_groups=mesh['dp'=24,'seq'=32] {'seq'}, dimensions={2}, use_global_device_ids=true | all-gather | bytes 33792 | tf_op jit(solution)/shard_map/all_gather | solution.py:116
  403.4 0.6 broadcast_multiply_fusion.2
  404.2 44.1 %all_gather.14 = f32[1,2,5120]{1,0,2:T(1,128)S(1)} all-gather(f32[1,2,160]{1,0,2:T(1,128)S(1)} %copy.61), channel_id=1, replica_groups=mesh['dp'=24,'seq'=32] {'seq'}, dimensions={2}, use_global_device_ids=true | all-gather | bytes 42240 | tf_op jit(solution)/shard_map/all_gather | solution.py:115
  448.4 3.2 copy.62
  (39 shorter events, 2.8 us)
Async XLA Ops:
  26.7 16.0 %copy-start.1 = (bf16[1,1,128,4096]{3,2,1,0:T(8,128)(2,1)S(1)}, bf16[1,1,128,4096]{3,2,1,0:T(8,128)(2,1)}, u32[]{:S(2)}) copy-start(bf16[1,1,128,4096]{3,2,1,0:T(8,128)(2,1)} %param.8) | copy-start | bytes 3145732
  27.9 15.6 %copy-start.3 = (bf16[1,2,5120]{2,1,0:T(2,128)(2,1)S(1)}, bf16[1,2,5120]{2,1,0:T(2,128)(2,1)}, u32[]{:S(2)}) copy-start(bf16[1,2,5120]{2,1,0:T(2,128)(2,1)} %param.11) | copy-start | bytes 61444
  27.9 15.6 %copy-start.5 = (s32[3,1,128]{2,1,0:T(1,128)S(1)}, s32[3,1,128]{2,1,0:T(1,128)}, u32[]{:S(2)}) copy-start(s32[3,1,128]{2,1,0:T(1,128)} %param.14) | copy-start | bytes 4612
  27.9 85.4 %all-to-all-start = ((bf16[32,2,8192]{2,1,0:T(2,128)(2,1)}), bf16[32,2,8192]{2,1,0:T(2,128)(2,1)}, u32[]{:S(2)}, u32[]{:S(2)}) async-start(bf16[32,2,8192]{2,1,0:T(2,128)(2,1)} %reshape.387), calls=%async_computation | async-start | bytes 2097152 | tf_op jit(solution)/shard_map/all_to_all | solution.py:98
  42.8 1.6 copy-start.6
  121.6 1.6 copy-start.2
  124.5 1.3 copy-start
  129.3 15.6 %copy-start.4 = (bf16[1,2,4096]{2,1,0:T(2,128)(2,1)S(1)}, bf16[1,2,4096]{2,1,0:T(2,128)(2,1)}, u32[]{:S(2)}) copy-start(bf16[1,2,4096]{2,1,0:T(2,128)(2,1)} %param.12) | copy-start | bytes 49156
  129.3 72.0 %all-to-all-start.2 = ((f32[32,1,48,128]{3,2,1,0:T(8,128)}), f32[32,1,48,128]{3,2,1,0:T(8,128)}, u32[]{:S(2)}, u32[]{:S(2)}) async-start(f32[32,1,48,128]{3,2,1,0:T(8,128)} %convolution_bitcast_fusion.1), calls=%async_computation.2 | async-start | bytes 1572864 | tf_op jit(solution)/shard_map/all_to_all | solution.py:20
  201.4 151.3 %all-to-all-start.1 = ((f32[32,1,48,160]{3,2,1,0:T(8,128)}), f32[32,1,48,160]{3,2,1,0:T(8,128)S(1)}, u32[]{:S(2)}, u32[]{:S(2)}) async-start(f32[32,1,48,160]{3,2,1,0:T(8,128)} %convolution_bitcast_fusion), calls=%async_computation.1 | async-start | bytes 3145728 | tf_op jit(solution)/shard_map/all_to_all | solution.py:20
  353.5 15.8 %all-to-all-start.3 = ((f32[24,1,2,288]{3,2,1,0:T(2,128)}), f32[24,1,2,288]{3,2,1,0:T(2,128)S(1)}, u32[]{:S(2)}, u32[]{:S(2)}) async-start(f32[24,1,2,288]{3,2,1,0:T(2,128)} %pad_maximum_fusion.1), calls=%async_computation.3 | async-start | bytes 147456 | tf_op jit(solution)/shard_map/all_to_all | solution.py:20
where the time goes:
time: 457 us; the launch traced here: 452 us
  blocking collectives  331 us (72%)
  starting transfers between devices  50 us (11%)
  other arithmetic  30.8 us (7%)
  local copies, waits for them, and re-layouts  20.7 us (5%)
  waiting for transfers between devices  10.6 us (2%)
  matrix products  7.35 us (2%)
    psum x1, blocking collectives, packed_total(): running = lax.psum(jnp.concatenate([a.ravel() for a in arrays]), axis)  131 us
    all_gather x1, blocking collectives, shards(): lax.all_gather(adapter_lowering, 'dp', axis=1, tiled=True)  68.8 us
    all_gather x1, blocking collectives, shards(): lax.all_gather(adapter_raising, 'dp', axis=1, tiled=True)  52.5 us
    all_gather x1, blocking collectives, shards(): lax.all_gather(down_share, 'seq', axis=2, tiled=True)  44.1 us
    all_to_all x3, starting transfers between devices, summed_on_arrival(): blocks = lax.all_to_all(cut_along(x, dim, count), axis, 0, 0, tiled=True)  35.1 us
    all_gather x1, blocking collectives, shards(): lax.all_gather(up_share, 'seq', axis=2, tiled=True)  34 us
    unnamed x1, other arithmetic  22.4 us
    unnamed x23, local copies, waits for them, and re-layouts  15.2 us
  transfers between devices with their start and end apart: 4, of which 1 were waited for; matrix products, arithmetic and copies ran while one was open for 2% of the time, Pallas kernels for 0%

commit v1 on v0

v1 whole, which is shorter than its diff:
```python
import jax
import jax.numpy as jnp
import numpy as np
from jax import lax
from jax.experimental import pallas as pl
from jax.experimental.pallas import tpu as pltpu
from jax.sharding import PartitionSpec as P

HD = 128
EPSILON = 1e-06
F32 = jnp.float32
BF16 = jnp.bfloat16

REM = 16


def onto(shape, dim):
    return lax.broadcasted_iota(jnp.int32, shape, dim)


def nt(a, b):
    return lax.dot_general(a, b, (((1,), (1,)), ((), ())), preferred_element_type=F32)


def nn(a, b):
    return lax.dot_general(a, b, (((1,), (0,)), ((), ())), preferred_element_type=F32)


def rope_tables(positions, valid):
    one_sixth = HD // 6
    counts = (HD // 2 - 2 * one_sixth, one_sixth, one_sixth)
    group = np.repeat(np.concatenate([np.full(n, k) for k, n in enumerate(counts)]), 2)
    powers = np.concatenate([-np.arange(n) / n for n in counts])
    frequency = np.repeat((10000.0**powers).astype(np.float32), 2)
    sign = np.where(np.arange(HD) % 2 == 0, 1.0, -1.0).astype(np.float32)
    at = positions.astype(F32)
    index = jnp.where(group == 0, at[0][:, None], jnp.where(group == 1, at[1][:, None], at[2][:, None]))
    angles = index * frequency
    keep = valid.astype(F32)[:, None]
    return jnp.cos(angles) * keep, jnp.sin(angles) * (keep * sign)


def prepare_kernel(proj, act, low, inverse, reduced):
    tokens, features = proj.shape

    def squares(h, acc):
        p = proj[:, pl.ds(pl.multiple_of(h * HD, HD), HD)].astype(F32)
        return acc + p * p

    acc = lax.fori_loop(0, features // HD, squares, jnp.zeros((tokens, HD), F32), unroll=4)
    mean = jnp.sum(acc, axis=1, keepdims=True) / features
    inverse[...] = jnp.broadcast_to(lax.rsqrt(mean + EPSILON), (tokens, HD))
    reduced[...] = nt(low[...], act[...]).astype(BF16)


def main_kernel(core, tg, proj, act, rai, inverse, reduced, cosine, sine, gains, valid, mine, theirs, scaled, delta, gain, rems):
    heads, tokens, _ = tg.shape
    features = heads * HD
    ranks = rai.shape[0]
    quarter = ranks // 4
    swap = (onto((HD, HD), 0) == (onto((HD, HD), 1) ^ 1)).astype(F32).astype(BF16)

    def first(h, acc):
        at = pl.ds(pl.multiple_of(h * HD, HD), HD)
        g = tg[h]
        unrotated = cosine[...] * g.astype(F32) + sine[...] * nn(g, swap)
        t = unrotated * (proj[:, at].astype(F32) * inverse[...])
        gain[h] = jnp.sum(t.reshape(tokens // 8, 8, HD), axis=0)
        gh = gains[:, at]
        scaled[h] = unrotated * gh
        return acc + t * gh

    acc = lax.fori_loop(0, heads, first, jnp.zeros((tokens, HD), F32), unroll=2)
    mean = jnp.broadcast_to(jnp.sum(acc, axis=1, keepdims=True) / features, (tokens, HD))

    def second(h, _):
        at = pl.ds(pl.multiple_of(h * HD, HD), HD)
        inv = inverse[...]
        normed = proj[:, at].astype(F32) * inv
        delta[:, at] = (inv * (scaled[h] - normed * mean)).astype(BF16)
        return 0

    lax.fori_loop(0, heads, second, 0, unroll=2)
    back = nt(rai[...], delta[...]).astype(BF16)
    for q in range(4):
        r = onto((REM, ranks), 0)
        pick = ((onto((REM, ranks), 1) == r + q * quarter) & (r < quarter)).astype(F32).astype(BF16)
        rems[q] = nn(pick, back).astype(BF16)
    up = reduced[...]
    count = jnp.sum(valid[...].astype(F32))
    c = core[0]

    def block(s, i, out):
        at = pl.ds(pl.multiple_of(s * HD, HD), HD)
        out[i, 0:ranks, :] = nn(up, delta[:, at]).astype(out.dtype)
        out[i, ranks : 2 * ranks, :] = nn(back, act[:, at]).astype(out.dtype)
        over = pl.ds(pl.multiple_of(features + (s // 4) * HD, HD), HD)
        rest = nn(rems[s % 4], act[:, over])
        row = onto((REM, HD), 0)
        g = jnp.sum(gain[s], axis=0, keepdims=True)
        rest = jnp.where(row == quarter, g, jnp.where(row == quarter + 1, count, rest))
        out[i, 2 * ranks : 2 * ranks + REM, :] = rest.astype(out.dtype)

    def pair(i, _):
        block(2 * i + c, i, mine)
        block(2 * i + 1 - c, i, theirs)
        return 0

    lax.fori_loop(0, heads // 2, pair, 0)


def spread_kernel(place, blocks, out, total, ranks, dp):
    peers, rows, _ = blocks.shape
    acc = blocks[0].astype(F32)
    for i in range(1, peers):
        acc = acc + blocks[i].astype(F32)
    total[...] = jnp.zeros_like(total)
    total[0:rows, :] = acc
    q = place[0]
    quarter = ranks // 4
    shape = (8 * dp, total.shape[0])
    r, k = onto(shape, 0), onto(shape, 1)
    j = r % 8
    at = 2 * (r // 8) + j % 2
    want = jnp.where(j < 2, at, at + ranks)
    rem = jnp.where(at // quarter == q, 2 * ranks + at % quarter, -1)
    want = jnp.where(j < 4, want, rem)
    want = jnp.where(j < 6, want, 2 * ranks + quarter + j - 6)
    pick = (k == want).astype(F32)
    out[...] = lax.dot_general(
        pick, total[...], (((1,), (0,)), ((), ())), precision=lax.Precision.HIGHEST, preferred_element_type=F32
    )


def finish_kernel(parts, down, up, gain, tokens):
    heads = parts.shape[0]
    factor = tokens / parts[0, 7:8, 0:1]
    for s in range(heads):
        b = parts[s] * factor
        up[:, s * HD : (s + 1) * HD] = b[0:2]
        down[:, s * HD : (s + 1) * HD] = b[2:4]
        gain[:, s * HD : (s + 1) * HD] = b[6:7]
    for t in range(heads // 4):
        b = parts[4 * t] + parts[4 * t + 1] + parts[4 * t + 2] + parts[4 * t + 3]
        down[:, (heads + t) * HD : (heads + t + 1) * HD] = b[4:6] * factor


VMEM = pl.BlockSpec(memory_space=pltpu.VMEM)
SMEM = pl.BlockSpec(memory_space=pltpu.SMEM)


def gather_ranks(adapter_lowering, adapter_raising, dp, seq):
    low_width = adapter_lowering.shape[2]
    own = jnp.concatenate([adapter_lowering[0], adapter_raising[0]], axis=1)
    full = lax.all_to_all(jnp.broadcast_to(own, (dp,) + own.shape), "dp", 0, 0, tiled=True)
    full = full.reshape(dp * own.shape[0], own.shape[1])
    return full[:, :low_width], full[:, low_width:]


def shards(projections, rotated_query_gradient, gains, adapter_lowering, adapter_raising, activations, positions, valid):
    dp, seq = lax.axis_size("dp"), lax.axis_size("seq")
    proj, act = projections[0, 0], activations[0]
    tokens, features = proj.shape
    ranks = dp * adapter_lowering.shape[1]
    member = lax.axis_index("seq")
    tg = rotated_query_gradient.reshape(seq, tokens, HD)
    tg = lax.all_to_all(tg, "seq", 0, 0, tiled=True)
    low, rai = gather_ranks(adapter_lowering, adapter_raising, dp, seq)
    cosine, sine = rope_tables(positions[:, 0], valid[0])
    inverse, reduced = pl.pallas_call(
        prepare_kernel,
        out_shape=(jax.ShapeDtypeStruct((tokens, HD), F32), jax.ShapeDtypeStruct((ranks, tokens), BF16)),
        in_specs=[VMEM] * 3,
        out_specs=(VMEM, VMEM),
    )(proj, act, low)
    rows = 2 * ranks + REM
    core = (member % 2).astype(jnp.int32).reshape(1)
    mine, theirs = pl.pallas_call(
        main_kernel,
        out_shape=(
            jax.ShapeDtypeStruct((seq // 2, rows, HD), F32),
            jax.ShapeDtypeStruct((seq // 2, rows, HD), BF16),
        ),
        in_specs=[SMEM] + [VMEM] * 10,
        out_specs=(VMEM, VMEM),
        scratch_shapes=[
            pltpu.VMEM((seq, tokens, HD), F32),
            pltpu.VMEM((tokens, features), BF16),
            pltpu.VMEM((seq, 8, HD), F32),
            pltpu.VMEM((4, REM, tokens), BF16),
        ],
    )(core, tg, proj, act, rai, inverse, reduced, cosine, sine, gains, valid)
    partner = lax.ppermute(theirs, "seq", [(s, s ^ 1) for s in range(seq)])
    both = (mine + partner.astype(F32)).astype(BF16)
    same_core = [[2 * i + c for i in range(seq // 2)] for c in range(2)]
    blocks = lax.all_to_all(both, "seq", 0, 0, tiled=True, axis_index_groups=same_core)
    place = (member % 4).astype(jnp.int32).reshape(1)
    rank_rows = pl.pallas_call(
        lambda *refs: spread_kernel(*refs, ranks=ranks, dp=dp),
        out_shape=jax.ShapeDtypeStruct((8 * dp, HD), F32),
        in_specs=[SMEM, VMEM],
        out_specs=VMEM,
        scratch_shapes=[pltpu.VMEM((128, HD), F32)],
    )(place, blocks)
    shares = lax.all_to_all(rank_rows.reshape(dp, 8, HD), "dp", 0, 0, tiled=True)
    share = jnp.sum(shares, axis=0)
    parts = lax.all_to_all(jnp.broadcast_to(share, (seq, 8, HD)), "seq", 0, 0, tiled=True)
    down, up, gain = pl.pallas_call(
        lambda *refs: finish_kernel(*refs, tokens=float(dp * seq * tokens)),
        out_shape=(
            jax.ShapeDtypeStruct((2, act.shape[1]), F32),
            jax.ShapeDtypeStruct((2, features), F32),
            jax.ShapeDtypeStruct((1, features), F32),
        ),
        in_specs=[VMEM],
        out_specs=(VMEM, VMEM, VMEM),
    )(parts)
    return down[None], up[None], gain


def solution(mesh):
    in_specs = (
        P(None, "dp", "seq", None),
        P(None, "dp", None, "seq"),
        P(),
        P(None, "dp", None),
        P(None, "dp", None),
        P("dp", "seq", None),
        P(None, "dp", "seq"),
        P("dp", "seq"),
    )
    out_specs = (P(None, "dp", None), P(None, "dp", None), P())
    return jax.shard_map(shards, mesh=mesh, in_specs=in_specs, out_specs=out_specs, check_vma=False)
```

time: 457 us -> 168 us (0.37); the launches traced: 452 us -> 168 us
  blocking collectives: 331 us -> 86.4 us
  starting transfers between devices: 50 us -> 16.6 us
  waiting for transfers between devices: 10.6 us -> 38.2 us
  other arithmetic: 30.8 us -> 3.86 us
  Pallas kernels: 0 us -> 17.6 us
  local copies, waits for them, and re-layouts: 20.7 us -> 4.18 us
  matrix products: 7.35 us -> 0 us
    all_gather x4 -> x0, blocking collectives: 199 us -> none  [the longest x1 68.8 us: shards(): lax.all_gather(adapter_lowering, 'dp', axis=1, tiled=True)]
    psum x1 -> x0, blocking collectives: 131 us -> none  [packed_total(): running = lax.psum(jnp.concatenate([a.ravel() for a in arrays]), axis)]
    all_to_all x0 -> x3, blocking collectives: none -> 86.4 us  [the longest x1 54 us: gather_ranks(): lax.all_to_all(jnp.broadcast_to(own, (dp,) + own.shape), 'dp', 0, 0, tile...]
    all_to_all x4 -> x2, starting transfers between devices: 50 us -> 13.9 us  [the longest x1 10.4 us: shards(): tg = lax.all_to_all(tg, 'seq', 0, 0, tiled=True)]
    all_to_all x4 -> x2, waiting for transfers between devices: 10.6 us -> 36.6 us  [the longest x1 21.8 us: shards(): tg = lax.all_to_all(tg, 'seq', 0, 0, tiled=True)]
    unnamed x1 -> x0, other arithmetic: 22.4 us -> none
    pallas_call x0 -> x4, Pallas kernels: none -> 17.6 us  [the longest x1 10.7 us: shards(): pl.pallas_call(main_kernel, out_shape=(jax.ShapeDtypeStruct((seq // 2, ro...]
    unnamed x23 -> x16, local copies, waits for them, and re-layouts: 15.2 us -> 1.77 us
  transfers between devices with their start and end apart: 4 -> 3, of which waited for: 1 -> 3; matrix products, arithmetic and copies ran while one was open for 2% -> 2% of each run, Pallas kernels for 0% -> 2%
where the time goes in v1:
time: 168 us
  blocking collectives  86.4 us (51%)
  waiting for transfers between devices  38.2 us (23%)
  Pallas kernels  17.6 us (10%)
  starting transfers between devices  16.6 us (10%)
  local copies, waits for them, and re-layouts  4.18 us (2%)
  other arithmetic  3.86 us (2%)
    all_to_all x1, blocking collectives, gather_ranks(): lax.all_to_all(jnp.broadcast_to(own, (dp,) + own.shape), 'dp', 0, 0, tile...  54 us
    all_to_all x1, waiting for transfers between devices, shards(): tg = lax.all_to_all(tg, 'seq', 0, 0, tiled=True)  21.8 us
    all_to_all x1, blocking collectives, shards(): lax.all_to_all(jnp.broadcast_to(share, (seq, 8, HD)), 'seq', 0, 0, tiled=...  16.7 us
    all_to_all x1, blocking collectives, shards(): lax.all_to_all(rank_rows.reshape(dp, 8, HD), 'dp', 0, 0, tiled=True)  15.6 us
    all_to_all x1, waiting for transfers between devices, shards(): lax.all_to_all(both, 'seq', 0, 0, tiled=True, axis_index_groups=same_core)  14.8 us
    pallas_call x1, Pallas kernels, shards(): pl.pallas_call(main_kernel, out_shape=(jax.ShapeDtypeStruct((seq // 2, ro...  10.7 us
    all_to_all x1, starting transfers between devices, shards(): tg = lax.all_to_all(tg, 'seq', 0, 0, tiled=True)  10.4 us
    all_to_all x1, starting transfers between devices, shards(): lax.all_to_all(both, 'seq', 0, 0, tiled=True, axis_index_groups=same_core)  3.56 us
  transfers between devices with their start and end apart: 3, of which 3 were waited for; matrix products, arithmetic and copies ran while one was open for 2% of the time, Pallas kernels for 2%

profile of v1, /device:TPU:1, one launch (start us, length us, event | category | flops | bytes accessed | tf_op | source)
XLA Modules:
  0.0 167.5 jit_solution(10055303986511795241)
XLA Ops:
  0.6 0.8 pad_maximum_fusion
  1.4 0.5 broadcast_in_dim.53
  1.9 54.0 %all_to_all.25 = bf16[24,2,9216]{2,1,0:T(2,128)(2,1)S(1)} all-to-all(bf16[24,2,9216]{2,1,0:T(2,128)(2,1)S(1)} %broadcast_in_dim.53), channel_id=1, replica_groups=mesh['dp'=24,'seq'=32] {'dp'}, dimensions={0} | all-to-all | bytes 1769472 | tf_op jit(solution)/shard_map/all_to_all | solution.py:155
  55.9 0.0 copy-start.2
  55.9 0.0 copy-start.7
  55.9 0.0 copy-start.5
  55.9 0.0 copy-start.6
  55.9 10.4 %all-to-all-start = ((bf16[32,128,128]{2,1,0:T(8,128)(2,1)}), bf16[32,128,128]{2,1,0:T(8,128)(2,1)S(1)}, u32[]{:S(2)}, u32[]{:S(2)}) async-start(bf16[32,128,128]{2,1,0:T(8,128)(2,1)} %bitcast.2), calls=%async_computation | async-start | bytes 2097152 | tf_op jit(solution)/shard_map/all_to_all | solution.py:167
  66.3 0.0 copy-done.2
  66.3 0.0 copy-done.7
  66.4 0.0 copy-done.3
  66.4 0.0 copy-done.4
  66.4 0.0 copy-done.5
  66.4 0.0 copy-done.6
  66.4 1.0 multiply_multiply_fusion
  67.4 0.3 reshape.42
  67.8 0.8 slice.23.rai
  68.5 0.8 slice.24.low
  69.4 3.2 %shard_map.139 = (f32[128,128]{1,0:T(8,128)}, bf16[48,128]{1,0:T(8,128)(2,1)}) custom-call(bf16[128,4096]{1,0:T(8,128)(2,1)} %bitcast.20, bf16[128,5120]{1,0:T(8,128)(2,1)} %bitcast.18, bf16[48,5120]{1,0:T(8,128)(2,1)} %slice.24.low), custom_call_target="tpu_custom_call" | custom-call | tf_op jit(solution)/shard_map/pallas_call | solution.py:170
  72.6 21.8 %all-to-all-done.tg = bf16[32,128,128]{2,1,0:T(8,128)(2,1)S(1)} async-done(((bf16[32,128,128]{2,1,0:T(8,128)(2,1)}), bf16[32,128,128]{2,1,0:T(8,128)(2,1)S(1)}, u32[]{:S(2)}, u32[]{:S(2)}) %all-to-all-start) | async-done | bytes 1048608 | tf_op jit(solution)/shard_map/all_to_all | solution.py:167
  94.4 1.0 copy-done
  95.4 10.7 %shard_map.140 = (f32[16,112,128]{2,1,0:T(8,128)}, bf16[16,112,128]{2,1,0:T(8,128)(2,1)}) custom-call(s32[1]{0:T(128)} %bitcast.1.core, bf16[32,128,128]{2,1,0:T(8,128)(2,1)} %copy-done, bf16[128,4096]{1,0:T(8,128)(2,1)} %bitcast.21, bf16[128,5120]{1,0:T(8,128)(2,1)} %bitcast.19, bf16[48,4096]{1,0:T(8,128)(2,1)} %slice.23.rai, ...), custom_call_target="tpu_custom_call" | custom-call | tf_op jit(solution)/shard_map/pallas_call | solution.py:178
  106.0 2.6 %collective-permute-start = (bf16[16,112,128]{2,1,0:T(8,128)(2,1)}, bf16[16,112,128]{2,1,0:T(8,128)(2,1)S(1)}, u32[]{:S(2)}, u32[]{:S(2)}) collective-permute-start(bf16[16,112,128]{2,1,0:T(8,128)(2,1)} %get-tuple-element.13), channel_id=1, source_target_pairs={{0,1},{1,0},{2,3},{3,2},{4,5},{5,4},{6,7},{7,6},{8,9},{9,8},{10,11... | collective-permute-start | bytes 1376264 | tf_op jit(solution)/shard_map/ppermute | solution.py:193
  108.7 1.6 collective-permute-done
  110.3 2.0 %add_convert_fusion = bf16[16,112,128]{2,1,0:T(8,128)(2,1)} fusion(f32[16,112,128]{2,1,0:T(8,128)} %get-tuple-element.12, bf16[16,112,128]{2,1,0:T(8,128)(2,1)S(1)} %collective-permute-done), kind=kLoop, calls=%fused_computation | loop fusion | flops 688128 | bytes 1835008 | tf_op jit(solution)/shard_map/convert_element_type | solution.py:194
  112.3 3.6 %all-to-all-start.2 = ((bf16[16,112,128]{2,1,0:T(8,128)(2,1)}), bf16[16,112,128]{2,1,0:T(8,128)(2,1)S(1)}, u32[]{:S(2)}, u32[]{:S(2)}) async-start(bf16[16,112,128]{2,1,0:T(8,128)(2,1)} %add_convert_fusion), calls=%async_computation.2 | async-start | bytes 917504 | tf_op jit(solution)/shard_map/all_to_all | solution.py:196
  115.9 14.8 %all-to-all-done.2.refs_1_ = bf16[16,112,128]{2,1,0:T(8,128)(2,1)S(1)} async-done(((bf16[16,112,128]{2,1,0:T(8,128)(2,1)}), bf16[16,112,128]{2,1,0:T(8,128)(2,1)S(1)}, u32[]{:S(2)}, u32[]{:S(2)}) %all-to-all-start.2) | async-done | bytes 458784 | tf_op jit(solution)/shard_map/all_to_all | solution.py:196
  130.7 0.8 copy-done.1
  131.5 2.1 %shard_map.141 = f32[192,128]{1,0:T(8,128)} custom-call(s32[1]{0:T(128)} %bitcast.refs_0_, bf16[16,112,128]{2,1,0:T(8,128)(2,1)} %copy-done.1), custom_call_target="tpu_custom_call" | custom-call | tf_op jit(solution)/shard_map/pallas_call | solution.py:198
  133.5 15.6 %all_to_all.26 = f32[24,8,128]{2,1,0:T(8,128)S(1)} all-to-all(f32[24,8,128]{2,1,0:T(8,128)} %bitcast.22), channel_id=1, replica_groups=mesh['dp'=24,'seq'=32] {'dp'}, dimensions={0} | all-to-all | bytes 196608 | tf_op jit(solution)/shard_map/all_to_all | solution.py:205
  149.2 16.7 %all_to_all.27.refs_0_ = f32[32,8,128]{2,1,0:T(8,128)} all-to-all(f32[32,8,128]{2,1,0:T(8,128)S(1)} %broadcast_in_dim.62), channel_id=1, replica_groups=mesh['dp'=24,'seq'=32] {'seq'}, dimensions={0} | all-to-all | bytes 262144 | tf_op jit(solution)/shard_map/all_to_all | solution.py:207
  165.9 1.6 shard_map.142
  (9 shorter events, 0.1 us)
Async XLA Ops:
  55.9 10.4 %copy-start.2 = (s32[3,1,128]{2,1,0:T(1,128)S(1)}, s32[3,1,128]{2,1,0:T(1,128)}, u32[]{:S(2)}) copy-start(s32[3,1,128]{2,1,0:T(1,128)} %param.18) | copy-start | bytes 4612
  55.9 10.4 %copy-start.7 = (s32[1,128]{1,0:T(1,128)S(1)}, s32[1,128]{1,0:T(1,128)}, u32[]{:S(2)}) copy-start(s32[1,128]{1,0:T(1,128)} %valid.1) | copy-start | bytes 1540
  55.9 10.5 %copy-start.3 = (f32[128]{0:T(128)S(1)}, f32[128]{0:T(128)}, u32[]{:S(2)}) copy-start(f32[128]{0:T(128)} %constant.40.clone) | copy-start | bytes 1540
  55.9 10.5 %copy-start.4 = (f32[128]{0:T(128)S(1)}, f32[128]{0:T(128)}, u32[]{:S(2)}) copy-start(f32[128]{0:T(128)} %constant.39.clone) | copy-start | bytes 1540
  55.9 10.5 %copy-start.5 = (pred[128]{0:T(512)(128)(4,1)S(1)}, pred[128]{0:T(512)(128)(4,1)}, u32[]{:S(2)}) copy-start(pred[128]{0:T(512)(128)(4,1)} %constant.38.clone) | copy-start | bytes 388
  55.9 10.5 %copy-start.6 = (pred[128]{0:T(512)(128)(4,1)S(1)}, pred[128]{0:T(512)(128)(4,1)}, u32[]{:S(2)}) copy-start(pred[128]{0:T(512)(128)(4,1)} %constant.37.clone) | copy-start | bytes 388
  55.9 38.4 %all-to-all-start = ((bf16[32,128,128]{2,1,0:T(8,128)(2,1)}), bf16[32,128,128]{2,1,0:T(8,128)(2,1)S(1)}, u32[]{:S(2)}, u32[]{:S(2)}) async-start(bf16[32,128,128]{2,1,0:T(8,128)(2,1)} %bitcast.2), calls=%async_computation | async-start | bytes 2097152 | tf_op jit(solution)/shard_map/all_to_all | solution.py:167
  94.4 1.0 copy-start
  106.0 4.3 %collective-permute-start = (bf16[16,112,128]{2,1,0:T(8,128)(2,1)}, bf16[16,112,128]{2,1,0:T(8,128)(2,1)S(1)}, u32[]{:S(2)}, u32[]{:S(2)}) collective-permute-start(bf16[16,112,128]{2,1,0:T(8,128)(2,1)} %get-tuple-element.13), channel_id=1, source_target_pairs={{0,1},{1,0},{2,3},{3,2},{4,5},{5,4},{6,7},{7,6},{8,9},{9,8},{10,11... | collective-permute-start | bytes 1376264 | tf_op jit(solution)/shard_map/ppermute | solution.py:193
  112.3 18.4 %all-to-all-start.2 = ((bf16[16,112,128]{2,1,0:T(8,128)(2,1)}), bf16[16,112,128]{2,1,0:T(8,128)(2,1)S(1)}, u32[]{:S(2)}, u32[]{:S(2)}) async-start(bf16[16,112,128]{2,1,0:T(8,128)(2,1)} %add_convert_fusion), calls=%async_computation.2 | async-start | bytes 917504 | tf_op jit(solution)/shard_map/all_to_all | solution.py:196
  130.7 0.8 copy-start.1
